TPU v7x, 8 devices: a whole 2x2x1 slice. The times are simulated.
8 devices in a mesh: nodes: 8 (over z, y, x, core).
Axes of the slice: x: 2, y: 2, z: 1, core: 2. Of those that a mesh axis runs over, the one named last changes fastest.
Arguments:
- adjacency: bfloat16 [16384, 16384], P('nodes')
- features: bfloat16 [16384, 128], P('nodes')
- w_one: float32 [128, 256], replicated
- w_two: float32 [256, 40], replicated
- labels: int32 [16384], P('nodes')
- label_mask: int32 [16384], P('nodes')
Outputs:
- output 1: float32 [1], replicated
- output 2: float32 [128, 256], replicated
- output 3: float32 [256, 40], replicated
All inputs are finite; a program needn't handle non-finite values.
Results may differ from a plain program's by a relative error of at most 0.001.
Values are sent between devices in bfloat16 or wider.
A program may use at most 1 GiB of HBM per device.

v0:
```python
import jax
import jax.numpy as jnp
from jax import lax
from jax.sharding import PartitionSpec as P

ROW_CONTRACT = (((0,), (0,)), ((), ()))
COL_CONTRACT = (((1,), (1,)), ((), ()))


def solution(mesh):
    axis_name = 'nodes'

    def local_step(adj_rows, feat_rows, w_one, w_two, label_rows, mask_rows):
        weight_one = w_one.astype(jnp.bfloat16)
        weight_two = w_two.astype(jnp.bfloat16)
        num_classes = w_two.shape[1]
        feats_all = lax.all_gather(feat_rows, axis_name, tiled=True)
        agg_one = jnp.dot(adj_rows, feats_all, preferred_element_type=jnp.float32).astype(jnp.bfloat16)
        pre_one = jnp.dot(agg_one, weight_one, preferred_element_type=jnp.float32)
        hidden = jnp.maximum(pre_one, 0.0).astype(jnp.bfloat16)
        hidden_all = lax.all_gather(hidden, axis_name, tiled=True)
        agg_two = jnp.dot(adj_rows, hidden_all, preferred_element_type=jnp.float32).astype(jnp.bfloat16)
        logits = jnp.dot(agg_two, weight_two, preferred_element_type=jnp.float32)
        weight = mask_rows.astype(jnp.float32)
        label_count = lax.psum(jnp.sum(weight), axis_name)
        onehot = (label_rows[:, None] == jnp.arange(num_classes)[None, :]).astype(jnp.float32)
        log_prob = jax.nn.log_softmax(logits, axis=-1)
        loss_sum = lax.psum(-jnp.sum(weight * jnp.sum(onehot * log_prob, axis=-1)), axis_name)
        grad_two = (weight[:, None] * (jnp.exp(log_prob) - onehot) / label_count).astype(jnp.bfloat16)
        dw_two = lax.psum(lax.dot_general(agg_two, grad_two, ROW_CONTRACT, preferred_element_type=jnp.float32), axis_name)
        back_two = lax.dot_general(grad_two, weight_two, COL_CONTRACT, preferred_element_type=jnp.float32).astype(jnp.bfloat16)
        part_sums = lax.dot_general(adj_rows, back_two, ROW_CONTRACT, preferred_element_type=jnp.float32)
        d_hidden = lax.psum_scatter(part_sums, axis_name, scatter_dimension=0, tiled=True)
        grad_one = jnp.where(pre_one > 0.0, d_hidden, 0.0).astype(jnp.bfloat16)
        dw_one = lax.psum(lax.dot_general(agg_one, grad_one, ROW_CONTRACT, preferred_element_type=jnp.float32), axis_name)
        return ((loss_sum / label_count).reshape(1), dw_one, dw_two)

    return jax.shard_map(local_step, mesh=mesh, in_specs=(P(axis_name, None), P(axis_name, None), P(None, None), P(None, None), P(axis_name), P(axis_name)), out_specs=(P(None), P(None, None), P(None, None)), check_vma=False)
```

profile of v0, /device:TPU:0, one launch (start us, length us, event | category | flops | bytes accessed | tf_op | source)
XLA Modules:
  0.0 375.4 jit_solution(922142295947725849)
XLA Ops:
  7.2 0.0 all-gather.3.cloned.1.call-start
  7.2 0.7 all-gather.3.cloned.1.call-update
  7.9 0.0 copy-start
  7.9 0.0 copy-start.2
  7.9 0.0 all-gather.5.cloned.1.call-start
  8.0 35.4 %all-gather.3.cloned.1.call-done = bf16[16384,128]{1,0:T(8,128)(2,1)} async-done(((bf16[2048,128]{1,0:T(8,128)(2,1)}), bf16[16384,128]{1,0:T(8,128)(2,1)}) %all-gather.3.cloned.1.call-update) | async-done | bytes 4194320 | tf_op jit(solution)/shard_map/all_gather | solution.py:17
  43.4 27.9 %convolution_convert_fusion.2 = bf16[2048,128]{1,0:T(8,128)(2,1)S(1)} fusion(bf16[2048,16384]{1,0:T(8,128)(2,1)} %param.6, bf16[16384,128]{1,0:T(8,128)(2,1)} %all-gather.3.cloned.1.call-done), kind=kOutput, calls=%fused_computation.3 | convolution fusion | flops 8590196736 | bytes 71827456 | tf_op jit(solution)/shard_map/dot_general | solution.py:18
  71.3 0.0 copy-done
  71.4 1.5 maximum_convert_fusion
  72.9 0.0 all-gather.5.cloned.1.call-update
  72.9 0.0 reduce-scatter.2.cloned.1.call-start
  72.9 0.0 copy-done.2
  73.0 0.0 copy-start.1
  73.0 0.0 copy-start.3
  73.0 48.4 %all-gather.5.cloned.1.call-done = bf16[16384,256]{1,0:T(8,128)(2,1)} async-done(((bf16[2048,256]{1,0:T(8,128)(2,1)}), bf16[16384,256]{1,0:T(8,128)(2,1)}) %all-gather.5.cloned.1.call-update) | async-done | bytes 8388624 | tf_op jit(solution)/shard_map/all_gather | solution.py:21
  121.4 28.5 %convolution_convert_fusion.1 = bf16[256,2048]{1,0:T(8,128)(2,1)} fusion(bf16[16384,256]{1,0:T(8,128)(2,1)} %all-gather.5.cloned.1.call-done, bf16[2048,16384]{1,0:T(8,128)(2,1)} %param.6), kind=kOutput, calls=%fused_computation.2 | convolution fusion | flops 17180393472 | bytes 76546048 | tf_op jit(solution)/shard_map/dot_general | solution.py:22
  149.9 0.0 copy-done.1
  149.9 1.5 fusion.10
  151.4 0.1 exponential_reduce_fusion
  151.5 0.1 select_reduce_fusion
  151.6 0.6 convert_reduce_fusion
  152.2 22.6 %psum.29 = f32[]{:T(128)} all-reduce(f32[]{:T(128)} %get-tuple-element.3), channel_id=1, replica_groups=mesh['nodes'=8] {'nodes'}, use_global_device_ids=true, to_apply=%region_6.7 | all-reduce | flops 1 | bytes 8 | tf_op jit(solution)/shard_map/psum | solution.py:25
  174.8 36.8 %convolution_bitcast_fusion = f32[16384,256]{1,0:T(8,128)} fusion(bf16[2048,16384]{1,0:T(8,128)(2,1)} %param.6, f32[256,40]{0,1:T(8,128)S(1)} %copy-done.1, f32[2048,40]{0,1:T(8,128)S(1)} %get-tuple-element.10, f32[]{:T(128)} %psum.29, f32[2048]{0:T(1024)S(1)} %convert_element_type.31, f32[2048]{0:T(1024)S(1)} %log.9, f32[2048]{0:T(1024)S(1)} %get-tuple-element.9, ...), kind=kOutput, calls=%fused_computation | convolution fusion | flops 17223002112 | bytes 84287488 | tf_op jit(solution)/shard_map/dot_general | solution.py:32
  211.5 0.0 reduce-scatter.2.cloned.1.call-update
  211.6 0.0 all-reduce.3.cloned.1.call-start
  211.6 109.0 %reduce-scatter.2.cloned.1.call-done = f32[2048,256]{1,0:T(8,128)} async-done(((f32[16384,256]{1,0:T(8,128)}), f32[2048,256]{1,0:T(8,128)}) %reduce-scatter.2.cloned.1.call-update) | async-done | bytes 2097168 | tf_op jit(solution)/shard_map/reduce_scatter | solution.py:33
  320.6 2.6 fusion
  323.2 0.0 all-reduce.3.cloned.1.call-update
  323.2 2.3 fusion.9
  326.2 23.2 %all-reduce = (f32[]{:T(128)}, f32[256,40]{0,1:T(8,128)}) all-reduce(f32[]{:T(128)S(6)} %neg.3, f32[256,40]{0,1:T(8,128)S(1)} %fusion.9), channel_id=1, replica_groups=mesh['nodes'=8] {'nodes'}, use_global_device_ids=true, to_apply=%region_4.5 | all-reduce | flops 10241 | bytes 81928 | tf_op jit(solution)/shard_map/psum | solution.py:28
  350.6 15.6 %all-reduce.3.cloned.1.call-done = f32[128,256]{1,0:T(8,128)} async-done(((f32[128,256]{1,0:T(8,128)}), f32[128,256]{1,0:T(8,128)}) %all-reduce.3.cloned.1.call-update) | async-done | bytes 131088 | tf_op jit(solution)/shard_map/psum | solution.py:35
  366.2 1.6 copy.10
  (3 shorter events, 0.0 us)
Async XLA Ops:
  7.2 36.2 %all-gather.3.cloned.1.call-start = ((), (), s32[]{:S(2)}) async-start(), calls=%async_computation.1 | async-start | bytes 4718592 | tf_op jit(solution)/shard_map/all_gather | solution.py:17
  7.9 63.4 %copy-start = (f32[128,256]{1,0:T(8,128)S(1)}, f32[128,256]{1,0:T(8,128)}, u32[]{:S(2)}) copy-start(f32[128,256]{1,0:T(8,128)} %param.8) | copy-start | bytes 393220
  7.9 65.0 %copy-start.2 = (s32[2048]{0:T(1024)S(1)}, s32[2048]{0:T(1024)}, u32[]{:S(2)}) copy-start(s32[2048]{0:T(1024)} %param.11) | copy-start | bytes 24580
  7.9 113.4 %all-gather.5.cloned.1.call-start = ((), (), s32[]{:S(2)}) async-start(), calls=%async_computation.2 | async-start | bytes 9437184 | tf_op jit(solution)/shard_map/all_gather | solution.py:21
  72.9 247.7 %reduce-scatter.2.cloned.1.call-start = ((), (), s32[]{:S(2)}) async-start(), calls=%async_computation.3 | async-start | bytes 18874368 | tf_op jit(solution)/shard_map/reduce_scatter | solution.py:33
  73.0 76.9 %copy-start.1 = (f32[256,40]{0,1:T(8,128)S(1)}, f32[256,40]{0,1:T(8,128)}, u32[]{:S(2)}) copy-start(f32[256,40]{0,1:T(8,128)} %param.9) | copy-start | bytes 122884
  73.0 78.5 %copy-start.3 = (s32[2048]{0:T(1024)S(1)}, s32[2048]{0:T(1024)}, u32[]{:S(2)}) copy-start(s32[2048]{0:T(1024)} %param.10) | copy-start | bytes 24580
  211.6 154.6 %all-reduce.3.cloned.1.call-start = ((), (), s32[]{:S(2)}) async-start(), calls=%async_computation.4 | async-start | bytes 262144 | tf_op jit(solution)/shard_map/psum | solution.py:35
Sparse Core Ops, SparseCore 0:
  9.8 33.5 all-gather.2
  73.0 48.3 all-gather.4
  211.7 108.8 reduce-scatter.1
  324.0 42.1 all-reduce.2
where the time goes:
time: 376 us; the launch traced here: 375 us
  waiting for transfers between devices  209 us (56%)
  matrix products  101 us (27%)
  blocking collectives  45.8 us (12%)
  between operations  16.9 us (4%)
    reduce_scatter x1, waiting for transfers between devices, local_step(): lax.psum_scatter(part_sums, axis_name, scatter_dimension=0, tiled=True)  109 us
    all_gather x1, waiting for transfers between devices, local_step(): hidden_all = lax.all_gather(hidden, axis_name, tiled=True)  48.4 us
    dot_general x1, matrix products, local_step(): lax.dot_general(adj_rows, back_two, ROW_CONTRACT, preferred_element_type=...  36.8 us
    all_gather x1, waiting for transfers between devices, local_step(): feats_all = lax.all_gather(feat_rows, axis_name, tiled=True)  35.4 us
    dot_general x1, matrix products, local_step(): jnp.dot(adj_rows, hidden_all, preferred_element_type=jnp.float32)  28.5 us
    dot_general x1, matrix products, local_step(): jnp.dot(adj_rows, feats_all, preferred_element_type=jnp.float32)  27.9 us
    psum x1, blocking collectives, local_step(): lax.psum(-jnp.sum(weight * jnp.sum(onehot * log_prob, axis=-1)), axis_name)  23.2 us
    psum x1, blocking collectives, local_step(): label_count = lax.psum(jnp.sum(weight), axis_name)  22.6 us
  transfers between devices with their start and end apart: 4, of which 4 were waited for; matrix products, arithmetic and copies ran while one was open for 1% of the time, Pallas kernels for 0%

commit v1 on v0

v1 whole, which is shorter than its diff:
```python
import functools

import jax
import jax.numpy as jnp
from jax import lax
from jax.experimental import pallas as pl
from jax.experimental.pallas import tpu as pltpu
from jax.sharding import PartitionSpec as P

AXIS = "nodes"
MESH = pl.DeviceIdType.MESH
F32 = jnp.float32
BF16 = jnp.bfloat16

SLOTS = 3
M_CHUNK = 512


def _dot(a, b):
    return jnp.dot(a, b, preferred_element_type=F32)


def _dot_nt(a, b):
    return lax.dot_general(a, b, (((1,), (1,)), ((), ())), preferred_element_type=F32)


def _kernel(
    adj, feat, w_one, w_two, labels, mask,
    out_loss, out_one, out_two,
    feats_all, aggs_all, hid, acc_one, acc_two, agg_two, back_t, grad_t, pre_t,
    own_sums, stage, from_pair, from_chip, adj_ring,
    w_one_f, w_two_f, w_one_b, w_one_t, w_two_b, w_two_t, lab_v, mask_v, count, count_in,
    red, red_pair, red_link, red_next, red_last, red_out,
    adj_sem, load_sem, gather_send, gather_recv, count_send, count_recv,
    pair_send, pair_recv, chip_send, chip_recv, red_send, red_recv,
):
    rows = feat.shape[0]
    half_rows, quarter = rows // 2, rows // 4
    classes = w_two.shape[1]
    me = lax.axis_index(AXIS)
    core, chip_x, chip_y = lax.rem(me, 2), lax.rem(me // 2, 2), me // 4
    to_pair, to_x, to_y = 1 - 2 * core, 2 - 4 * chip_x, 4 - 8 * chip_y
    pair, x_next, y_next = me + to_pair, me + to_x, me + to_y

    def remote(src, dst, send, recv, dev):
        return pltpu.make_async_remote_copy(
            src_ref=src, dst_ref=dst, send_sem=send, recv_sem=recv, device_id=(dev,), device_id_type=MESH)

    def gather_place(s):
        flip = lax.rem(s // 2, 2)
        far = s // 12
        near = (s + 12) // 16 - far
        along_y = lax.rem(s, 2)
        second = (s // 8) * (1 - far)
        blk = me + flip * to_pair + (near * (1 - along_y) + far) * to_x + (near * along_y + far) * to_y
        return blk, lax.rem(s + second, 2)

    def reduce_place(u):
        own = u // 12
        diag = 1 - (u + 12) // 16
        link = lax.rem(u, 2)
        nx = (1 - own) * (diag + (1 - diag) * (1 - link))
        ny = (1 - own) * (diag + (1 - diag) * link)
        part = own * (u - 12) + (1 - own) * (2 * lax.rem(link + u // 8, 2) + lax.rem(u // 2, 2))
        return me + nx * to_x + ny * to_y, part

    def slab_copy(n):
        blk, half = gather_place(lax.rem(n, 16))
        col = pl.multiple_of(blk * rows + half * half_rows, half_rows)
        slot = lax.rem(n, SLOTS)
        return pltpu.make_async_copy(adj.at[:, pl.ds(col, half_rows)], adj_ring.at[slot], adj_sem.at[slot, 0])

    def part_copy(n, which):
        blk, part = reduce_place(n - 32)
        blk = blk + to_pair * (1 - which)
        col = pl.multiple_of(blk * rows + part * quarter, quarter)
        slot = lax.rem(n, SLOTS)
        return pltpu.make_async_copy(
            adj.at[:, pl.ds(col, quarter)],
            adj_ring.at[slot, :, pl.ds(which * quarter, quarter)], adj_sem.at[slot, which])

    def fetch(n):
        @pl.when(n < 32)
        def _():
            slab_copy(n).start()

        @pl.when((n >= 32) & (n < 48))
        def _():
            part_copy(n, 0).start()
            part_copy(n, 1).start()

    loads = [
        pltpu.make_async_copy(feat, feats_all.at[me], load_sem.at[0]),
        pltpu.make_async_copy(mask, mask_v, load_sem.at[1]),
        pltpu.make_async_copy(w_one, w_one_f, load_sem.at[2]),
        pltpu.make_async_copy(w_two, w_two_f, load_sem.at[3]),
        pltpu.make_async_copy(labels, lab_v, load_sem.at[4]),
    ]
    for load in loads:
        load.start()
    for n in range(SLOTS):
        slab_copy(n).start()

    barrier = pltpu.get_barrier_semaphore()
    for dev in (pair, x_next, y_next):
        pl.semaphore_signal(barrier, inc=1, device_id=(dev,), device_id_type=MESH)
    acc_one[...] = jnp.zeros_like(acc_one)
    acc_two[...] = jnp.zeros_like(acc_two)
    grad_t[...] = jnp.zeros_like(grad_t)
    pl.semaphore_wait(barrier, 3)

    def piece(buf, s):
        blk, half = gather_place(s)
        return buf.at[blk, pl.ds(pl.multiple_of(half * half_rows, half_rows), half_rows), :]

    def send_piece(ph, buf, s, to, dev):
        ref = piece(buf, s)
        return remote(ref, ref, gather_send.at[ph, to], gather_recv.at[ph, to], dev)

    def send_own(ph, buf, half):
        send_piece(ph, buf, half, 4 + 4 * half, x_next).start()
        send_piece(ph, buf, half, 9 - 4 * half, y_next).start()

    def gather_step(ph, buf, s):
        @pl.when(s >= 2)
        def _():
            send_piece(ph, buf, s, s, pair).wait_recv()

        @pl.when(s == 4)
        def _():
            send_piece(ph, buf, 4, 12, y_next).start()

        @pl.when(s == 5)
        def _():
            send_piece(ph, buf, 5, 13, x_next).start()

        @pl.when(lax.rem(s // 2, 2) == 0)
        def _():
            send_piece(ph, buf, s, s + 2, pair).start()

    def count_move(i):
        return remote(count.at[i], count_in.at[i], count_send.at[i], count_recv.at[i], (pair, x_next, y_next)[i])

    loads[0].wait()
    send_piece(0, feats_all, 0, 4, x_next).start()
    send_piece(0, feats_all, 1, 5, y_next).start()
    send_piece(0, feats_all, 1, 8, x_next).start()
    send_piece(0, feats_all, 0, 9, y_next).start()
    for load in loads[1:]:
        load.wait()
    count[0] = jnp.full((8, 128), jnp.sum(mask_v[...].astype(F32)), F32)
    count_move(0).start()
    w_one_b[...] = w_one_f[...].astype(BF16)
    w_one_t[...] = w_one_f[...].T.astype(BF16)
    w_two_b[...] = jnp.zeros_like(w_two_b)
    w_two_b[:, :classes] = w_two_f[...].astype(BF16)
    w_two_t[...] = w_two_b[...].astype(F32).T.astype(BF16)

    def step_one(s, carry):
        gather_step(0, feats_all, s)

        for i, when in enumerate((1, 12)):
            @pl.when(s == when)
            def _(i=i):
                count_move(i).wait_recv()
                count[i + 1] = count[i] + count_in[i]
                count_move(i + 1).start()

        slab_copy(s).wait()
        slot = lax.rem(s, SLOTS)
        right = piece(feats_all, s)[...]
        for m in range(0, rows, M_CHUNK):
            at = pl.ds(m, M_CHUNK)
            acc_one[at, :] += _dot(adj_ring[slot, at, :], right)
        fetch(s + SLOTS)
        return carry

    lax.fori_loop(0, 16, step_one, 0)

    aggs_all[me] = acc_one[...].astype(BF16)
    send_piece(1, aggs_all, 0, 4, x_next).start()
    send_piece(1, aggs_all, 1, 5, y_next).start()
    send_piece(1, aggs_all, 1, 8, x_next).start()
    send_piece(1, aggs_all, 0, 9, y_next).start()

    def step_two(s, carry):
        gather_step(1, aggs_all, s)
        hid[...] = jnp.maximum(_dot(piece(aggs_all, s)[...], w_one_b[...]), 0.0).astype(BF16)
        n = s + 16
        slab_copy(n).wait()
        slot = lax.rem(n, SLOTS)
        right = hid[...]
        for m in range(0, rows, M_CHUNK):
            at = pl.ds(m, M_CHUNK)
            acc_two[at, :] += _dot(adj_ring[slot, at, :], right)
        fetch(n + SLOTS)
        return carry

    lax.fori_loop(0, 16, step_two, 0)

    count_move(2).wait_recv()
    total = (count[2] + count_in[2])[0:1, 0:1]
    agg_two[...] = acc_two[...].astype(BF16)
    logits = _dot_nt(w_two_t[0:48, :], agg_two[...])[:classes, :]
    weight = mask_v[...].astype(F32)
    shifted = logits - jnp.max(logits, axis=0, keepdims=True)
    log_prob = shifted - jnp.log(jnp.sum(jnp.exp(shifted), axis=0, keepdims=True))
    onehot = (lax.broadcasted_iota(jnp.int32, (classes, rows), 0) == lab_v[...]).astype(F32)
    picked = jnp.sum(onehot * log_prob, axis=0, keepdims=True)
    loss_sum = -jnp.sum(weight * picked)
    grad_t[:classes, :] = (weight * (jnp.exp(log_prob) - onehot) / total).astype(BF16)
    back_t[...] = _dot(w_two_b[...], grad_t[...]).astype(BF16)

    def pair_move(u):
        return remote(stage.at[lax.rem(u, 4)], from_pair.at[u], pair_send.at[lax.rem(u, 4)], pair_recv.at[u], pair)

    def chip_move(u):
        link = lax.rem(u, 2)
        dev = me + (1 - link) * to_x + link * to_y
        return remote(own_sums.at[u], from_chip.at[link, u // 2], chip_send.at[u], chip_recv.at[link, u // 2], dev)

    def finish(u):
        pair_move(u).wait_recv()
        own_sums[u] += from_pair[u]

        @pl.when(u < 8)
        def _():
            chip_move(u).start()

    def step_three(u, carry):
        n = u + 32
        slot = lax.rem(n, SLOTS)

        @pl.when(u >= 4)
        def _():
            pair_move(u).wait_send()

        part_copy(n, 0).wait()
        stage[lax.rem(u, 4)] = _dot(back_t[...], adj_ring[slot, :, pl.ds(0, quarter)])
        pair_move(u).start()
        part_copy(n, 1).wait()
        own_sums[u] = _dot(back_t[...], adj_ring[slot, :, pl.ds(quarter, quarter)])
        fetch(n + SLOTS)

        @pl.when(u >= 1)
        def _():
            finish(u - 1)

        return carry

    lax.fori_loop(0, 16, step_three, 0)
    finish(jnp.int32(15))
    for u in range(12, 16):
        pair_move(u).wait_send()

    part_two = _dot(grad_t[0:48, :], agg_two[...])
    red[256:296, :] = part_two[0:classes, 0:128]
    red[296:336, :] = part_two[0:classes, 128:256]
    red[336:352, :] = jnp.full((16, 128), loss_sum, F32)
    pre_t[...] = _dot_nt(w_one_t[...], aggs_all[me])

    for k in range(2):
        for link in range(2):
            u = 8 + 2 * k + (1 - link)
            chip_move(2 * k + link).wait_recv()
            own_sums[u] += from_chip[link, k]
            chip_move(u).start()

    def part_of_one(j):
        return 12 + j

    for k in range(2):
        for link in range(2):
            j = 2 * link + k
            chip_move(4 + 2 * k + link).wait_recv()
            own_sums[12 + j] += from_chip[link, 2 + k]
    red_one = jnp.zeros((256, 128), F32)
    for k in range(2):
        for link in range(2):
            j = 2 * (1 - link) + k
            chip_move(8 + 2 * k + link).wait_recv()
            d_hidden = own_sums[12 + j] + from_chip[link, 4 + k]
            keep = pre_t[:, pl.ds(j * quarter, quarter)] > 0.0
            grad_one = jnp.where(keep, d_hidden, 0.0).astype(BF16)
            red_one += _dot(grad_one, aggs_all[me, pl.ds(j * quarter, quarter), :])
    red[0:256, :] = red_one

    n_half = red.shape[0] // 2
    n_part = n_half // 2
    mine = pl.multiple_of(core * n_half, 8)
    other = pl.multiple_of((1 - core) * n_half, 8)

    move = remote(red.at[pl.ds(other, n_half)], red_pair, red_send.at[0], red_recv.at[0], pair)
    move.start()
    move.wait_recv()
    red_link[...] = red[pl.ds(mine, n_half), :] + red_pair[...]
    moves = [
        remote(red_link.at[pl.ds(i * n_part, n_part)], red_next.at[pl.ds(i * n_part, n_part)],
               red_send.at[1 + i], red_recv.at[1 + i], (x_next, y_next)[i])
        for i in range(2)
    ]
    for m in moves:
        m.start()
    for m in moves:
        m.wait_recv()
    red_pair2 = red_link[...] + red_next[...]
    red_last[0] = red_pair2
    lasts = [
        remote(red_last.at[0, pl.ds(i * n_part, n_part)], red_last.at[1, pl.ds(i * n_part, n_part)],
               red_send.at[3 + i], red_recv.at[3 + i], (y_next, x_next)[i])
        for i in range(2)
    ]
    for m in lasts:
        m.start()
    for m in lasts:
        m.wait_recv()
    red_out[pl.ds(mine, n_half), :] = red_last[0] + red_last[1]
    ref = red_out.at[pl.ds(mine, n_half)]
    back = remote(ref, ref, red_send.at[5], red_recv.at[5], pair)
    back.start()
    ref_in = red_out.at[pl.ds(other, n_half)]
    remote(ref_in, ref_in, red_send.at[5], red_recv.at[5], pair).wait_recv()

    out_one[...] = red_out[0:256, :].T
    out_two[0:128, :] = red_out[256:296, :].T
    out_two[128:256, :] = red_out[296:336, :].T
    out_loss[...] = red_out[336:337, 0:1] / total

    move.wait_send()
    for m in moves + lasts + [back]:
        m.wait_send()
    for i in range(3):
        count_move(i).wait_send()
    for ph, buf in ((0, feats_all), (1, aggs_all)):
        for to in range(2, 16):
            send_piece(ph, buf, to, to, pair).wait_send()
    for u in range(12):
        chip_move(u).wait_send()


def solution(mesh):
    def step(adj, feat, w_one, w_two, labels, mask):
        rows, nodes = adj.shape
        feat_dim, hidden = w_one.shape
        classes = w_two.shape[1]
        parts = nodes // rows
        any_spec = pl.BlockSpec(memory_space=pltpu.HBM)
        vmem = pl.BlockSpec(memory_space=pltpu.VMEM)
        quarter = rows // 4
        scratch = [
            pltpu.VMEM((parts, rows, feat_dim), BF16),
            pltpu.VMEM((parts, rows, feat_dim), BF16),
            pltpu.VMEM((rows // 2, hidden), BF16),
            pltpu.VMEM((rows, feat_dim), F32),
            pltpu.VMEM((rows, hidden), F32),
            pltpu.VMEM((rows, hidden), BF16),
            pltpu.VMEM((hidden, rows), BF16),
            pltpu.VMEM((128, rows), BF16),
            pltpu.VMEM((hidden, rows), F32),
            pltpu.VMEM((16, hidden, quarter), F32),
            pltpu.VMEM((4, hidden, quarter), F32),
            pltpu.VMEM((16, hidden, quarter), F32),
            pltpu.VMEM((2, 6, hidden, quarter), F32),
            pltpu.VMEM((SLOTS, rows, rows // 2), BF16),
            pltpu.VMEM((feat_dim, hidden), F32),
            pltpu.VMEM((hidden, classes), F32),
            pltpu.VMEM((feat_dim, hidden), BF16),
            pltpu.VMEM((hidden, feat_dim), BF16),
            pltpu.VMEM((hidden, 128), BF16),
            pltpu.VMEM((128, hidden), BF16),
            pltpu.VMEM((1, rows), jnp.int32),
            pltpu.VMEM((1, rows), jnp.int32),
            pltpu.VMEM((3, 8, 128), F32),
            pltpu.VMEM((3, 8, 128), F32),
            pltpu.VMEM((352, 128), F32),
            pltpu.VMEM((176, 128), F32),
            pltpu.VMEM((176, 128), F32),
            pltpu.VMEM((176, 128), F32),
            pltpu.VMEM((2, 176, 128), F32),
            pltpu.VMEM((352, 128), F32),
            pltpu.SemaphoreType.DMA((SLOTS, 2)),
            pltpu.SemaphoreType.DMA((5,)),
            pltpu.SemaphoreType.DMA((2, 16)),
            pltpu.SemaphoreType.DMA((2, 16)),
            pltpu.SemaphoreType.DMA((3,)),
            pltpu.SemaphoreType.DMA((3,)),
            pltpu.SemaphoreType.DMA((4,)),
            pltpu.SemaphoreType.DMA((16,)),
            pltpu.SemaphoreType.DMA((12,)),
            pltpu.SemaphoreType.DMA((2, 6)),
            pltpu.SemaphoreType.DMA((6,)),
            pltpu.SemaphoreType.DMA((6,)),
        ]
        loss, dw_one, dw_two = pl.pallas_call(
            _kernel,
            out_shape=(
                jax.ShapeDtypeStruct((1, 1), F32),
                jax.ShapeDtypeStruct((feat_dim, hidden), F32),
                jax.ShapeDtypeStruct((hidden, classes), F32),
            ),
            in_specs=[any_spec] * 6,
            out_specs=(vmem, vmem, vmem),
            scratch_shapes=scratch,
            compiler_params=pltpu.CompilerParams(
                collective_id=0, has_side_effects=True, vmem_limit_bytes=67_000_000),
            name="gcn_step",
        )(adj, feat, w_one, w_two, labels.reshape(1, rows), mask.reshape(1, rows))
        return loss.reshape(1), dw_one, dw_two

    return jax.shard_map(
        step,
        mesh=mesh,
        in_specs=(P(AXIS, None), P(AXIS, None), P(None, None), P(None, None), P(AXIS), P(AXIS)),
        out_specs=(P(None), P(None, None), P(None, None)),
        check_vma=False,
    )
```

time: 376 us -> 146 us (0.39)
  waiting for transfers between devices: 209 us -> 0 us
  Pallas kernels: 0 us -> 139 us
  matrix products: 101 us -> 0 us
  blocking collectives: 45.8 us -> 0 us
  between operations: 16.9 us -> 2.41 us
    pallas_call x0 -> x1, Pallas kernels: none -> 139 us  [step(): pl.pallas_call(_kernel, out_shape=(jax.ShapeDtypeStruct((1, 1), F32), jax...]
    reduce_scatter x1 -> x0, waiting for transfers between devices: 109 us -> none  [local_step(): lax.psum_scatter(part_sums, axis_name, scatter_dimension=0, tiled=True)]
    dot_general x7 -> x0, matrix products: 101 us -> none  [the longest x1 36.8 us: local_step(): lax.dot_general(adj_rows, back_two, ROW_CONTRACT, preferred_element_type=...]
    all_gather x2 -> x0, waiting for transfers between devices: 83.8 us -> none  [the longest x1 48.4 us: local_step(): hidden_all = lax.all_gather(hidden, axis_name, tiled=True)]
    psum x2 -> x0, blocking collectives: 45.8 us -> none  [the longest x1 23.2 us: local_step(): lax.psum(-jnp.sum(weight * jnp.sum(onehot * log_prob, axis=-1)), axis_name)]
    psum x1 -> x0, waiting for transfers between devices: 15.6 us -> none  [local_step(): lax.psum(lax.dot_general(agg_one, grad_one, ROW_CONTRACT, preferred_eleme...]
  transfers between devices with their start and end apart: 4 -> 0, of which waited for: 4 -> 0; matrix products, arithmetic and copies ran while one was open for 1% -> 0% of each run, Pallas kernels for 0% -> 0%
where the time goes in v1:
time: 146 us
  Pallas kernels  139 us (95%)
  local copies, waits for them, and re-layouts  4.7 us (3%)
  between operations  2.41 us (2%)
    pallas_call x1, Pallas kernels, step(): pl.pallas_call(_kernel, out_shape=(jax.ShapeDtypeStruct((1, 1), F32), jax...  139 us
    unnamed x3, local copies, waits for them, and re-layouts  4.7 us

profile of v1, /device:TPU:0, one launch (start us, length us, event | category | flops | bytes accessed | tf_op | source)
XLA Modules:
  0.0 146.1 jit_solution(5563956035981355782)
XLA Ops:
  0.6 1.5 %copy.9.w_two = f32[256,40]{1,0:T(8,128)} copy(f32[256,40]{0,1:T(8,128)} %param.9) | data formatting | bytes 81920 | tf_op args[3]
  2.2 139.0 %gcn_step.1 = (f32[1,1]{1,0:T(1,128)}, f32[128,256]{1,0:T(8,128)}, f32[256,40]{1,0:T(8,128)}) custom-call(bf16[2048,16384]{1,0:T(8,128)(2,1)} %adj.1, bf16[2048,128]{1,0:T(8,128)(2,1)} %feat.1, f32[128,256]{1,0:T(8,128)} %w_one.1, f32[256,40]{1,0:T(8,128)} %copy.9.w_two, s32[1,2048]{1,0:T(1,128)} %bitcast.3, s32[1,2048]{1,0:T(1,128)} %bitcast.4), custom_call_target="tpu_custom_call" | custom-call | tf_op jit(solution)/shard_map/gcn_step/pallas_call | solution.py:394
  141.2 1.6 %copy.10 = f32[256,40]{0,1:T(8,128)} copy(f32[256,40]{1,0:T(8,128)} %get-tuple-element.11) | data formatting | bytes 81920
  143.4 1.6 %copy.14 = f32[128,256]{1,0:T(8,128)} copy(f32[128,256]{1,0:T(8,128)} %get-tuple-element.16) | data formatting | bytes 262144

commit v2 on v1

--- a/solution.py
+++ b/solution.py
@@ -26,17 +26,17 @@
 
 def _kernel(
     adj, feat, w_one, w_two, labels, mask,
-    out_loss, out_one, out_two,
+    out,
     feats_all, aggs_all, hid, acc_one, acc_two, agg_two, back_t, grad_t, pre_t,
     own_sums, stage, from_pair, from_chip, adj_ring,
     w_one_f, w_two_f, w_one_b, w_one_t, w_two_b, w_two_t, lab_v, mask_v, count, count_in,
-    red, red_pair, red_link, red_next, red_last, red_out,
+    red, red_pair, red_link, red_next, red_last, red_out, small, small_in,
     adj_sem, load_sem, gather_send, gather_recv, count_send, count_recv,
-    pair_send, pair_recv, chip_send, chip_recv, red_send, red_recv,
+    pair_send, pair_recv, chip_send, chip_recv, red_send, red_recv, small_send, small_recv,
 ):
     rows = feat.shape[0]
-    half_rows, quarter = rows // 2, rows // 4
-    classes = w_two.shape[1]
+    quarter = rows // 4
+    classes = w_two.shape[0]
     me = lax.axis_index(AXIS)
     core, chip_x, chip_y = lax.rem(me, 2), lax.rem(me // 2, 2), me // 4
     to_pair, to_x, to_y = 1 - 2 * core, 2 - 4 * chip_x, 4 - 8 * chip_y
@@ -46,14 +46,14 @@
         return pltpu.make_async_remote_copy(
             src_ref=src, dst_ref=dst, send_sem=send, recv_sem=recv, device_id=(dev,), device_id_type=MESH)
 
-    def gather_place(s):
-        flip = lax.rem(s // 2, 2)
+    def gather_place(s, e):
+        low = 1 - (s + 12) // 16
         far = s // 12
-        near = (s + 12) // 16 - far
-        along_y = lax.rem(s, 2)
-        second = (s // 8) * (1 - far)
-        blk = me + flip * to_pair + (near * (1 - along_y) + far) * to_x + (near * along_y + far) * to_y
-        return blk, lax.rem(s + second, 2)
+        near = 1 - low - far
+        flip = low * (s // 2) + (1 - low) * lax.rem(s, 2)
+        blk = me + flip * to_pair + (near * (1 - e) + far) * to_x + (near * e + far) * to_y
+        part = (low * (2 * lax.rem(s, 2) + e) + near * lax.rem(s // 2 + 2 + 2 * e, 4) + far * (s // 2 - 6 + 2 * e))
+        return blk, part
 
     def reduce_place(u):
         own = u // 12
@@ -64,30 +64,30 @@
         part = own * (u - 12) + (1 - own) * (2 * lax.rem(link + u // 8, 2) + lax.rem(u // 2, 2))
         return me + nx * to_x + ny * to_y, part
 
-    def slab_copy(n):
-        blk, half = gather_place(lax.rem(n, 16))
-        col = pl.multiple_of(blk * rows + half * half_rows, half_rows)
-        slot = lax.rem(n, SLOTS)
-        return pltpu.make_async_copy(adj.at[:, pl.ds(col, half_rows)], adj_ring.at[slot], adj_sem.at[slot, 0])
-
-    def part_copy(n, which):
-        blk, part = reduce_place(n - 32)
-        blk = blk + to_pair * (1 - which)
+    def adj_copy(place, n, e):
+        blk, part = place
         col = pl.multiple_of(blk * rows + part * quarter, quarter)
         slot = lax.rem(n, SLOTS)
         return pltpu.make_async_copy(
-            adj.at[:, pl.ds(col, quarter)],
-            adj_ring.at[slot, :, pl.ds(which * quarter, quarter)], adj_sem.at[slot, which])
+            adj.at[:, pl.ds(col, quarter)], adj_ring.at[slot, :, pl.ds(e * quarter, quarter)], adj_sem.at[slot, e])
+
+    def slab_copy(n, e):
+        return adj_copy(gather_place(lax.rem(n, 16), e), n, e)
+
+    def part_copy(n, e):
+        blk, part = reduce_place(n - 32)
+        return adj_copy((blk + to_pair * (1 - e), part), n, e)
 
     def fetch(n):
         @pl.when(n < 32)
         def _():
-            slab_copy(n).start()
+            for e in range(2):
+                slab_copy(n, e).start()
 
         @pl.when((n >= 32) & (n < 48))
         def _():
-            part_copy(n, 0).start()
-            part_copy(n, 1).start()
+            for e in range(2):
+                part_copy(n, e).start()
 
     loads = [
         pltpu.make_async_copy(feat, feats_all.at[me], load_sem.at[0]),
@@ -99,7 +99,8 @@
     for load in loads:
         load.start()
     for n in range(SLOTS):
-        slab_copy(n).start()
+        for e in range(2):
+            slab_copy(n, e).start()
 
     barrier = pltpu.get_barrier_semaphore()
     for dev in (pair, x_next, y_next):
@@ -109,52 +110,55 @@
     grad_t[...] = jnp.zeros_like(grad_t)
     pl.semaphore_wait(barrier, 3)
 
-    def piece(buf, s):
-        blk, half = gather_place(s)
-        return buf.at[blk, pl.ds(pl.multiple_of(half * half_rows, half_rows), half_rows), :]
-
-    def send_piece(ph, buf, s, to, dev):
-        ref = piece(buf, s)
-        return remote(ref, ref, gather_send.at[ph, to], gather_recv.at[ph, to], dev)
-
-    def send_own(ph, buf, half):
-        send_piece(ph, buf, half, 4 + 4 * half, x_next).start()
-        send_piece(ph, buf, half, 9 - 4 * half, y_next).start()
+    def piece(buf, s, e):
+        blk, part = gather_place(s, e)
+        return buf.at[blk, pl.ds(pl.multiple_of(part * quarter, quarter), quarter), :]
+
+    def send_piece(ph, buf, s, e, to, dev):
+        ref = piece(buf, s, e)
+        at = 2 * to + e
+        return remote(ref, ref, gather_send.at[ph, at], gather_recv.at[ph, at], dev)
+
+    def send_own(ph, buf):
+        for i in range(4):
+            for e, dev in ((0, x_next), (1, y_next)):
+                part = (i + 2 * e) % 4
+                ref = buf.at[me, pl.ds(part * quarter, quarter), :]
+                at = 2 * (4 + 2 * i) + e
+                remote(ref, ref, gather_send.at[ph, at], gather_recv.at[ph, at], dev).start()
 
     def gather_step(ph, buf, s):
-        @pl.when(s >= 2)
-        def _():
-            send_piece(ph, buf, s, s, pair).wait_recv()
-
-        @pl.when(s == 4)
-        def _():
-            send_piece(ph, buf, 4, 12, y_next).start()
-
-        @pl.when(s == 5)
-        def _():
-            send_piece(ph, buf, 5, 13, x_next).start()
-
-        @pl.when(lax.rem(s // 2, 2) == 0)
-        def _():
-            send_piece(ph, buf, s, s + 2, pair).start()
+        for e in range(2):
+            @pl.when(s >= 2)
+            def _():
+                send_piece(ph, buf, s, e, s, pair).wait_recv()
+
+            @pl.when((s == 4) | (s == 6))
+            def _():
+                send_piece(ph, buf, s, e, s + 8, (y_next, x_next)[e]).start()
+
+            @pl.when(s < 2)
+            def _():
+                send_piece(ph, buf, s, e, s + 2, pair).start()
+
+            @pl.when((s >= 4) & (lax.rem(s, 2) == 0))
+            def _():
+                send_piece(ph, buf, s, e, s + 1, pair).start()
 
     def count_move(i):
         return remote(count.at[i], count_in.at[i], count_send.at[i], count_recv.at[i], (pair, x_next, y_next)[i])
 
     loads[0].wait()
-    send_piece(0, feats_all, 0, 4, x_next).start()
-    send_piece(0, feats_all, 1, 5, y_next).start()
-    send_piece(0, feats_all, 1, 8, x_next).start()
-    send_piece(0, feats_all, 0, 9, y_next).start()
+    send_own(0, feats_all)
     for load in loads[1:]:
         load.wait()
     count[0] = jnp.full((8, 128), jnp.sum(mask_v[...].astype(F32)), F32)
     count_move(0).start()
     w_one_b[...] = w_one_f[...].astype(BF16)
     w_one_t[...] = w_one_f[...].T.astype(BF16)
-    w_two_b[...] = jnp.zeros_like(w_two_b)
-    w_two_b[:, :classes] = w_two_f[...].astype(BF16)
-    w_two_t[...] = w_two_b[...].astype(F32).T.astype(BF16)
+    w_two_t[...] = jnp.zeros_like(w_two_t)
+    w_two_t[:classes, :] = w_two_f[...].astype(BF16)
+    w_two_b[...] = w_two_t[...].astype(F32).T.astype(BF16)
 
     def step_one(s, carry):
         gather_step(0, feats_all, s)
@@ -166,9 +170,10 @@
                 count[i + 1] = count[i] + count_in[i]
                 count_move(i + 1).start()
 
-        slab_copy(s).wait()
+        for e in range(2):
+            slab_copy(s, e).wait()
         slot = lax.rem(s, SLOTS)
-        right = piece(feats_all, s)[...]
+        right = jnp.concatenate([piece(feats_all, s, e)[...] for e in range(2)], axis=0)
         for m in range(0, rows, M_CHUNK):
             at = pl.ds(m, M_CHUNK)
             acc_one[at, :] += _dot(adj_ring[slot, at, :], right)
@@ -178,16 +183,16 @@
     lax.fori_loop(0, 16, step_one, 0)
 
     aggs_all[me] = acc_one[...].astype(BF16)
-    send_piece(1, aggs_all, 0, 4, x_next).start()
-    send_piece(1, aggs_all, 1, 5, y_next).start()
-    send_piece(1, aggs_all, 1, 8, x_next).start()
-    send_piece(1, aggs_all, 0, 9, y_next).start()
+    send_own(1, aggs_all)
 
     def step_two(s, carry):
         gather_step(1, aggs_all, s)
-        hid[...] = jnp.maximum(_dot(piece(aggs_all, s)[...], w_one_b[...]), 0.0).astype(BF16)
+        for e in range(2):
+            pre = _dot(piece(aggs_all, s, e)[...], w_one_b[...])
+            hid[pl.ds(e * quarter, quarter), :] = jnp.maximum(pre, 0.0).astype(BF16)
         n = s + 16
-        slab_copy(n).wait()
+        for e in range(2):
+            slab_copy(n, e).wait()
         slot = lax.rem(n, SLOTS)
         right = hid[...]
         for m in range(0, rows, M_CHUNK):
@@ -254,10 +259,19 @@
         pair_move(u).wait_send()
 
     part_two = _dot(grad_t[0:48, :], agg_two[...])
-    red[256:296, :] = part_two[0:classes, 0:128]
-    red[296:336, :] = part_two[0:classes, 128:256]
-    red[336:352, :] = jnp.full((16, 128), loss_sum, F32)
+    small[0, 0:40, :] = part_two[0:classes, 0:128]
+    small[0, 40:80, :] = part_two[0:classes, 128:256]
+    small[0, 80:96, :] = jnp.full((16, 128), loss_sum, F32)
+
+    def small_move(i):
+        return remote(small.at[i], small_in.at[i], small_send.at[i], small_recv.at[i], (pair, x_next, y_next)[i])
+
+    small_move(0).start()
     pre_t[...] = _dot_nt(w_one_t[...], aggs_all[me])
+
+    small_move(0).wait_recv()
+    small[1] = small[0] + small_in[0]
+    small_move(1).start()
 
     for k in range(2):
         for link in range(2):
@@ -266,14 +280,14 @@
             own_sums[u] += from_chip[link, k]
             chip_move(u).start()
 
-    def part_of_one(j):
-        return 12 + j
-
     for k in range(2):
         for link in range(2):
             j = 2 * link + k
             chip_move(4 + 2 * k + link).wait_recv()
             own_sums[12 + j] += from_chip[link, 2 + k]
+    small_move(1).wait_recv()
+    small[2] = small[1] + small_in[1]
+    small_move(2).start()
     red_one = jnp.zeros((256, 128), F32)
     for k in range(2):
         for link in range(2):
@@ -283,7 +297,7 @@
             keep = pre_t[:, pl.ds(j * quarter, quarter)] > 0.0
             grad_one = jnp.where(keep, d_hidden, 0.0).astype(BF16)
             red_one += _dot(grad_one, aggs_all[me, pl.ds(j * quarter, quarter), :])
-    red[0:256, :] = red_one
+    red[...] = red_one
 
     n_half = red.shape[0] // 2
     n_part = n_half // 2
@@ -321,21 +335,32 @@
     ref_in = red_out.at[pl.ds(other, n_half)]
     remote(ref_in, ref_in, red_send.at[5], red_recv.at[5], pair).wait_recv()
 
-    out_one[...] = red_out[0:256, :].T
-    out_two[0:128, :] = red_out[256:296, :].T
-    out_two[128:256, :] = red_out[296:336, :].T
-    out_loss[...] = red_out[336:337, 0:1] / total
+    small_move(2).wait_recv()
+    summed = small[2] + small_in[2]
+    out[0:256, :] = red_out[...]
+    out[256:336, :] = summed[0:80, :]
+    out[336:352, :] = summed[80:96, :] / total
 
     move.wait_send()
     for m in moves + lasts + [back]:
         m.wait_send()
     for i in range(3):
         count_move(i).wait_send()
+        small_move(i).wait_send()
     for ph, buf in ((0, feats_all), (1, aggs_all)):
         for to in range(2, 16):
-            send_piece(ph, buf, to, to, pair).wait_send()
+            for e in range(2):
+                send_piece(ph, buf, to, e, to, pair).wait_send()
     for u in range(12):
         chip_move(u).wait_send()
+
+
+def _finish(sums, out_loss, out_one, out_two):
+    classes = out_two.shape[0]
+    out_one[...] = sums[0:256, :].T
+    out_two[:, 0:128] = sums[256:256 + classes, :]
+    out_two[:, 128:256] = sums[256 + classes:256 + 2 * classes, :]
+    out_loss[...] = sums[336:337, 0:1]
 
 
 def solution(mesh):
@@ -363,7 +388,7 @@
             pltpu.VMEM((2, 6, hidden, quarter), F32),
             pltpu.VMEM((SLOTS, rows, rows // 2), BF16),
             pltpu.VMEM((feat_dim, hidden), F32),
-            pltpu.VMEM((hidden, classes), F32),
+            pltpu.VMEM((classes, hidden), F32),
             pltpu.VMEM((feat_dim, hidden), BF16),
             pltpu.VMEM((hidden, feat_dim), BF16),
             pltpu.VMEM((hidden, 128), BF16),
@@ -372,16 +397,18 @@
             pltpu.VMEM((1, rows), jnp.int32),
             pltpu.VMEM((3, 8, 128), F32),
             pltpu.VMEM((3, 8, 128), F32),
-            pltpu.VMEM((352, 128), F32),
-            pltpu.VMEM((176, 128), F32),
-            pltpu.VMEM((176, 128), F32),
-            pltpu.VMEM((176, 128), F32),
-            pltpu.VMEM((2, 176, 128), F32),
-            pltpu.VMEM((352, 128), F32),
+            pltpu.VMEM((256, 128), F32),
+            pltpu.VMEM((128, 128), F32),
+            pltpu.VMEM((128, 128), F32),
+            pltpu.VMEM((128, 128), F32),
+            pltpu.VMEM((2, 128, 128), F32),
+            pltpu.VMEM((256, 128), F32),
+            pltpu.VMEM((3, 96, 128), F32),
+            pltpu.VMEM((3, 96, 128), F32),
             pltpu.SemaphoreType.DMA((SLOTS, 2)),
             pltpu.SemaphoreType.DMA((5,)),
-            pltpu.SemaphoreType.DMA((2, 16)),
-            pltpu.SemaphoreType.DMA((2, 16)),
+            pltpu.SemaphoreType.DMA((2, 32)),
+            pltpu.SemaphoreType.DMA((2, 32)),
             pltpu.SemaphoreType.DMA((3,)),
             pltpu.SemaphoreType.DMA((3,)),
             pltpu.SemaphoreType.DMA((4,)),
@@ -390,22 +417,31 @@
             pltpu.SemaphoreType.DMA((2, 6)),
             pltpu.SemaphoreType.DMA((6,)),
             pltpu.SemaphoreType.DMA((6,)),
+            pltpu.SemaphoreType.DMA((3,)),
+            pltpu.SemaphoreType.DMA((3,)),
         ]
-        loss, dw_one, dw_two = pl.pallas_call(
+        sums = pl.pallas_call(
             _kernel,
-            out_shape=(
-                jax.ShapeDtypeStruct((1, 1), F32),
-                jax.ShapeDtypeStruct((feat_dim, hidden), F32),
-                jax.ShapeDtypeStruct((hidden, classes), F32),
-            ),
+            out_shape=jax.ShapeDtypeStruct((352, 128), F32),
             in_specs=[any_spec] * 6,
-            out_specs=(vmem, vmem, vmem),
+            out_specs=vmem,
             scratch_shapes=scratch,
             compiler_params=pltpu.CompilerParams(
                 collective_id=0, has_side_effects=True, vmem_limit_bytes=67_000_000),
             name="gcn_step",
-        )(adj, feat, w_one, w_two, labels.reshape(1, rows), mask.reshape(1, rows))
-        return loss.reshape(1), dw_one, dw_two
+        )(adj, feat, w_one, w_two.T, labels.reshape(1, rows), mask.reshape(1, rows))
+        loss, dw_one, dw_two_t = pl.pallas_call(
+            _finish,
+            out_shape=(
+                jax.ShapeDtypeStruct((1, 1), F32),
+                jax.ShapeDtypeStruct((feat_dim, hidden), F32),
+                jax.ShapeDtypeStruct((classes, hidden), F32),
+            ),
+            in_specs=[vmem],
+            out_specs=(vmem, vmem, vmem),
+            name="gcn_finish",
+        )(sums)
+        return loss.reshape(1), dw_one, dw_two_t.T
 
     return jax.shard_map(
         step,

time: 146 us -> 141 us (0.966)
  local copies, waits for them, and re-layouts: 4.7 us -> 0 us
  between operations: 2.41 us -> 0.64 us
    unnamed x3 -> x0, local copies, waits for them, and re-layouts: 4.7 us -> none
    pallas_call x1 -> x2, Pallas kernels: 139 us -> 140 us  [the longest x1 138 us: step(): pl.pallas_call(_kernel, out_shape=jax.ShapeDtypeStruct((352, 128), F32),...]
where the time goes in v2:
time: 141 us
  Pallas kernels  140 us (99%)
    pallas_call x1, Pallas kernels, step(): pl.pallas_call(_kernel, out_shape=jax.ShapeDtypeStruct((352, 128), F32),...  138 us

profile of v2, /device:TPU:0, one launch (start us, length us, event | category | flops | bytes accessed | tf_op | source)
XLA Modules:
  0.0 140.6 jit_solution(13929100893356707832)
XLA Ops:
  0.6 138.3 %gcn_step.1.sums = f32[352,128]{1,0:T(8,128)} custom-call(bf16[2048,16384]{1,0:T(8,128)(2,1)} %adj.1, bf16[2048,128]{1,0:T(8,128)(2,1)} %feat.1, f32[128,256]{1,0:T(8,128)} %w_one.1, f32[40,256]{1,0:T(8,128)} %bitcast.5, s32[1,2048]{1,0:T(1,128)} %bitcast.6, s32[1,2048]{1,0:T(1,128)} %bitcast.7), custom_call_target="tpu_custom_call" | custom-call | tf_op jit(solution)/shard_map/gcn_step/pallas_call | solution.py:423
  139.0 1.7 %gcn_finish.1 = (f32[1,1]{1,0:T(1,128)}, f32[128,256]{1,0:T(8,128)}, f32[40,256]{1,0:T(8,128)}) custom-call(f32[352,128]{1,0:T(8,128)} %gcn_step.1.sums), custom_call_target="tpu_custom_call" | custom-call | tf_op jit(solution)/shard_map/gcn_finish/pallas_call | solution.py:433

commit v3 on v2

--- a/solution.py
+++ b/solution.py
@@ -1,5 +1,3 @@
-import functools
-
 import jax
 import jax.numpy as jnp
 from jax import lax
@@ -28,11 +26,11 @@
     adj, feat, w_one, w_two, labels, mask,
     out,
     feats_all, aggs_all, hid, acc_one, acc_two, agg_two, back_t, grad_t, pre_t,
-    own_sums, stage, from_pair, from_chip, adj_ring,
+    own_part, own_sums, stage, from_pair, to_chip, from_chip, adj_buf,
     w_one_f, w_two_f, w_one_b, w_one_t, w_two_b, w_two_t, lab_v, mask_v, count, count_in,
     red, red_pair, red_link, red_next, red_last, red_out, small, small_in,
     adj_sem, load_sem, gather_send, gather_recv, count_send, count_recv,
-    pair_send, pair_recv, chip_send, chip_recv, red_send, red_recv, small_send, small_recv,
+    pair_send, pair_recv, pair_free, chip_send, chip_recv, red_send, red_recv, small_send, small_recv, relay_send,
 ):
     rows = feat.shape[0]
     quarter = rows // 4
@@ -58,36 +56,39 @@
     def reduce_place(u):
         own = u // 12
         diag = 1 - (u + 12) // 16
+        near = 1 - own - diag
         link = lax.rem(u, 2)
-        nx = (1 - own) * (diag + (1 - diag) * (1 - link))
-        ny = (1 - own) * (diag + (1 - diag) * link)
-        part = own * (u - 12) + (1 - own) * (2 * lax.rem(link + u // 8, 2) + lax.rem(u // 2, 2))
+        nx = diag + near * (1 - link)
+        ny = diag + near * link
+        part = own * (u - 12) + diag * (2 * link + u // 2) + near * (u // 2 - 2)
         return me + nx * to_x + ny * to_y, part
 
-    def adj_copy(place, n, e):
+    def adj_copy(place, slot, e):
         blk, part = place
         col = pl.multiple_of(blk * rows + part * quarter, quarter)
-        slot = lax.rem(n, SLOTS)
         return pltpu.make_async_copy(
-            adj.at[:, pl.ds(col, quarter)], adj_ring.at[slot, :, pl.ds(e * quarter, quarter)], adj_sem.at[slot, e])
-
-    def slab_copy(n, e):
-        return adj_copy(gather_place(lax.rem(n, 16), e), n, e)
-
-    def part_copy(n, e):
-        blk, part = reduce_place(n - 32)
-        return adj_copy((blk + to_pair * (1 - e), part), n, e)
-
-    def fetch(n):
-        @pl.when(n < 32)
+            adj.at[:, pl.ds(col, quarter)], adj_buf.at[slot, :, pl.ds(e * quarter, quarter)], adj_sem.at[slot, e])
+
+    def kept_copy(s, e):
+        return adj_copy(gather_place(s, e), SLOTS + s, e)
+
+    def slab_copy(r, e):
+        return adj_copy(gather_place(lax.rem(r, 12) + 4, e), lax.rem(r, SLOTS), e)
+
+    def part_copy(r, e):
+        blk, part = reduce_place(r - 24)
+        return adj_copy((blk + to_pair * (1 - e), part), lax.rem(r, SLOTS), e)
+
+    def fetch(r):
+        @pl.when((r >= SLOTS) & (r < 24))
         def _():
             for e in range(2):
-                slab_copy(n, e).start()
-
-        @pl.when((n >= 32) & (n < 48))
+                slab_copy(r, e).start()
+
+        @pl.when((r >= 24) & (r < 36))
         def _():
             for e in range(2):
-                part_copy(n, e).start()
+                part_copy(r, e).start()
 
     loads = [
         pltpu.make_async_copy(feat, feats_all.at[me], load_sem.at[0]),
@@ -98,6 +99,9 @@
     ]
     for load in loads:
         load.start()
+    for n in range(4):
+        for e in range(2):
+            kept_copy(n, e).start()
     for n in range(SLOTS):
         for e in range(2):
             slab_copy(n, e).start()
@@ -170,14 +174,15 @@
                 count[i + 1] = count[i] + count_in[i]
                 count_move(i + 1).start()
 
+        kept = 1 - (s + 12) // 16
+        slot = kept * (SLOTS + s) + (1 - kept) * lax.rem(s + 8, SLOTS)
         for e in range(2):
-            slab_copy(s, e).wait()
-        slot = lax.rem(s, SLOTS)
+            adj_copy(gather_place(s, e), slot, e).wait()
         right = jnp.concatenate([piece(feats_all, s, e)[...] for e in range(2)], axis=0)
         for m in range(0, rows, M_CHUNK):
             at = pl.ds(m, M_CHUNK)
-            acc_one[at, :] += _dot(adj_ring[slot, at, :], right)
-        fetch(s + SLOTS)
+            acc_one[at, :] += _dot(adj_buf[slot, at, :], right)
+        fetch(s - 4 + SLOTS)
         return carry
 
     lax.fori_loop(0, 16, step_one, 0)
@@ -185,22 +190,38 @@
     aggs_all[me] = acc_one[...].astype(BF16)
     send_own(1, aggs_all)
 
-    def step_two(s, carry):
-        gather_step(1, aggs_all, s)
+    def hidden_step(s):
         for e in range(2):
             pre = _dot(piece(aggs_all, s, e)[...], w_one_b[...])
-            hid[pl.ds(e * quarter, quarter), :] = jnp.maximum(pre, 0.0).astype(BF16)
-        n = s + 16
-        for e in range(2):
-            slab_copy(n, e).wait()
-        slot = lax.rem(n, SLOTS)
-        right = hid[...]
+            hid[lax.rem(s, 2), pl.ds(e * quarter, quarter), :] = jnp.maximum(pre, 0.0).astype(BF16)
+
+    def step_two(s, carry):
+        @pl.when(s < 15)
+        def _():
+            gather_step(1, aggs_all, s + 1)
+
+        kept = 1 - (s + 12) // 16
+        slot = kept * (SLOTS + s) + (1 - kept) * lax.rem(s + 8, SLOTS)
+
+        @pl.when(s >= 4)
+        def _():
+            for e in range(2):
+                adj_copy(gather_place(s, e), slot, e).wait()
+
+        hidden_step(jnp.minimum(s + 1, 15))
+        right = hid[lax.rem(s, 2)]
         for m in range(0, rows, M_CHUNK):
             at = pl.ds(m, M_CHUNK)
-            acc_two[at, :] += _dot(adj_ring[slot, at, :], right)
-        fetch(n + SLOTS)
+            acc_two[at, :] += _dot(adj_buf[slot, at, :], right)
+
+        @pl.when(s >= 4)
+        def _():
+            fetch(s + 8 + SLOTS)
+
         return carry
 
+    gather_step(1, aggs_all, jnp.int32(0))
+    hidden_step(jnp.int32(0))
     lax.fori_loop(0, 16, step_two, 0)
 
     count_move(2).wait_recv()
@@ -217,35 +238,53 @@
     back_t[...] = _dot(w_two_b[...], grad_t[...]).astype(BF16)
 
     def pair_move(u):
-        return remote(stage.at[lax.rem(u, 4)], from_pair.at[u], pair_send.at[lax.rem(u, 4)], pair_recv.at[u], pair)
+        at = lax.rem(u, 4)
+        return remote(stage.at[at], from_pair.at[at], pair_send.at[at], pair_recv.at[u], pair)
 
     def chip_move(u):
         link = lax.rem(u, 2)
         dev = me + (1 - link) * to_x + link * to_y
-        return remote(own_sums.at[u], from_chip.at[link, u // 2], chip_send.at[u], chip_recv.at[link, u // 2], dev)
+        return remote(to_chip.at[u], from_chip.at[link, u // 2], chip_send.at[u], chip_recv.at[link, u // 2], dev)
 
     def finish(u):
         pair_move(u).wait_recv()
-        own_sums[u] += from_pair[u]
-
-        @pl.when(u < 8)
-        def _():
+        both = own_part[lax.rem(u, 2)] + from_pair[lax.rem(u, 4)]
+
+        @pl.when(u < 12)
+        def _():
+            to_chip[u] = both.astype(BF16)
             chip_move(u).start()
+            pl.semaphore_signal(pair_free, inc=1, device_id=(pair,), device_id_type=MESH)
+
+        @pl.when(u >= 12)
+        def _():
+            own_sums[u - 12] = both
 
     def step_three(u, carry):
-        n = u + 32
-        slot = lax.rem(n, SLOTS)
+        r = u + 24
+        ring = 1 - u // 12
+        kept = (1 - ring) * (u - 12)
+        slots = [ring * lax.rem(r, SLOTS) + (1 - ring) * (SLOTS + 2 * (1 - e) + kept // 2) for e in range(2)]
+        cols = [pl.multiple_of((ring * e + lax.rem(kept, 2)) * quarter, quarter) for e in range(2)]
 
         @pl.when(u >= 4)
         def _():
             pair_move(u).wait_send()
-
-        part_copy(n, 0).wait()
-        stage[lax.rem(u, 4)] = _dot(back_t[...], adj_ring[slot, :, pl.ds(0, quarter)])
+            pl.semaphore_wait(pair_free, 1)
+
+        @pl.when(u < 12)
+        def _():
+            part_copy(r, 0).wait()
+
+        stage[lax.rem(u, 4)] = _dot(back_t[...], adj_buf[slots[0], :, pl.ds(cols[0], quarter)])
         pair_move(u).start()
-        part_copy(n, 1).wait()
-        own_sums[u] = _dot(back_t[...], adj_ring[slot, :, pl.ds(quarter, quarter)])
-        fetch(n + SLOTS)
+
+        @pl.when(u < 12)
+        def _():
+            part_copy(r, 1).wait()
+
+        own_part[lax.rem(u, 2)] = _dot(back_t[...], adj_buf[slots[1], :, pl.ds(cols[1], quarter)])
+        fetch(r + SLOTS)
 
         @pl.when(u >= 1)
         def _():
@@ -273,18 +312,19 @@
     small[1] = small[0] + small_in[0]
     small_move(1).start()
 
+    relays = []
     for k in range(2):
         for link in range(2):
-            u = 8 + 2 * k + (1 - link)
             chip_move(2 * k + link).wait_recv()
-            own_sums[u] += from_chip[link, k]
-            chip_move(u).start()
-
-    for k in range(2):
+            move = remote(from_chip.at[link, k], from_chip.at[1 - link, 6 + k], relay_send.at[link, k],
+                          chip_recv.at[1 - link, 6 + k], (y_next, x_next)[link])
+            move.start()
+            relays.append(move)
+
+    for j in range(4):
         for link in range(2):
-            j = 2 * link + k
-            chip_move(4 + 2 * k + link).wait_recv()
-            own_sums[12 + j] += from_chip[link, 2 + k]
+            chip_move(4 + 2 * j + link).wait_recv()
+            own_sums[j] += from_chip[link, 2 + j].astype(F32)
     small_move(1).wait_recv()
     small[2] = small[1] + small_in[1]
     small_move(2).start()
@@ -292,8 +332,8 @@
     for k in range(2):
         for link in range(2):
             j = 2 * (1 - link) + k
-            chip_move(8 + 2 * k + link).wait_recv()
-            d_hidden = own_sums[12 + j] + from_chip[link, 4 + k]
+            relays[2 * k + 1 - link].wait_recv()
+            d_hidden = own_sums[j] + from_chip[link, 6 + k].astype(F32)
             keep = pre_t[:, pl.ds(j * quarter, quarter)] > 0.0
             grad_one = jnp.where(keep, d_hidden, 0.0).astype(BF16)
             red_one += _dot(grad_one, aggs_all[me, pl.ds(j * quarter, quarter), :])
@@ -353,6 +393,8 @@
                 send_piece(ph, buf, to, e, to, pair).wait_send()
     for u in range(12):
         chip_move(u).wait_send()
+    for relay in relays:
+        relay.wait_send()
 
 
 def _finish(sums, out_loss, out_one, out_two):
@@ -375,18 +417,20 @@
         scratch = [
             pltpu.VMEM((parts, rows, feat_dim), BF16),
             pltpu.VMEM((parts, rows, feat_dim), BF16),
-            pltpu.VMEM((rows // 2, hidden), BF16),
+            pltpu.VMEM((2, rows // 2, hidden), BF16),
             pltpu.VMEM((rows, feat_dim), F32),
             pltpu.VMEM((rows, hidden), F32),
             pltpu.VMEM((rows, hidden), BF16),
             pltpu.VMEM((hidden, rows), BF16),
             pltpu.VMEM((128, rows), BF16),
             pltpu.VMEM((hidden, rows), F32),
-            pltpu.VMEM((16, hidden, quarter), F32),
+            pltpu.VMEM((2, hidden, quarter), F32),
             pltpu.VMEM((4, hidden, quarter), F32),
-            pltpu.VMEM((16, hidden, quarter), F32),
-            pltpu.VMEM((2, 6, hidden, quarter), F32),
-            pltpu.VMEM((SLOTS, rows, rows // 2), BF16),
+            pltpu.VMEM((4, hidden, quarter), F32),
+            pltpu.VMEM((4, hidden, quarter), F32),
+            pltpu.VMEM((12, hidden, quarter), BF16),
+            pltpu.VMEM((2, 8, hidden, quarter), BF16),
+            pltpu.VMEM((SLOTS + 4, rows, rows // 2), BF16),
             pltpu.VMEM((feat_dim, hidden), F32),
             pltpu.VMEM((classes, hidden), F32),
             pltpu.VMEM((feat_dim, hidden), BF16),
@@ -405,7 +449,7 @@
             pltpu.VMEM((256, 128), F32),
             pltpu.VMEM((3, 96, 128), F32),
             pltpu.VMEM((3, 96, 128), F32),
-            pltpu.SemaphoreType.DMA((SLOTS, 2)),
+            pltpu.SemaphoreType.DMA((SLOTS + 4, 2)),
             pltpu.SemaphoreType.DMA((5,)),
             pltpu.SemaphoreType.DMA((2, 32)),
             pltpu.SemaphoreType.DMA((2, 32)),
@@ -413,12 +457,14 @@
             pltpu.SemaphoreType.DMA((3,)),
             pltpu.SemaphoreType.DMA((4,)),
             pltpu.SemaphoreType.DMA((16,)),
+            pltpu.SemaphoreType.REGULAR,
             pltpu.SemaphoreType.DMA((12,)),
-            pltpu.SemaphoreType.DMA((2, 6)),
+            pltpu.SemaphoreType.DMA((2, 8)),
             pltpu.SemaphoreType.DMA((6,)),
             pltpu.SemaphoreType.DMA((6,)),
             pltpu.SemaphoreType.DMA((3,)),
             pltpu.SemaphoreType.DMA((3,)),
+            pltpu.SemaphoreType.DMA((2, 2)),
         ]
         sums = pl.pallas_call(
             _kernel,

time: 141 us -> 125 us (0.89)
  Pallas kernels: 140 us -> 125 us
    pallas_call x1, Pallas kernels: 138 us -> 123 us  [step(): pl.pallas_call(_kernel, out_shape=jax.ShapeDtypeStruct((352, 128), F32),...]
where the time goes in v3:
time: 125 us
  Pallas kernels  125 us (100%)
    pallas_call x1, Pallas kernels, step(): pl.pallas_call(_kernel, out_shape=jax.ShapeDtypeStruct((352, 128), F32),...  123 us

profile of v3, /device:TPU:0, one launch (start us, length us, event | category | flops | bytes accessed | tf_op | source)
XLA Modules:
  0.0 125.1 jit_solution(14234401462746323242)
XLA Ops:
  0.6 122.8 %gcn_step.1.sums = f32[352,128]{1,0:T(8,128)} custom-call(bf16[2048,16384]{1,0:T(8,128)(2,1)} %adj.1, bf16[2048,128]{1,0:T(8,128)(2,1)} %feat.1, f32[128,256]{1,0:T(8,128)} %w_one.1, f32[40,256]{1,0:T(8,128)} %bitcast.5, s32[1,2048]{1,0:T(1,128)} %bitcast.6, s32[1,2048]{1,0:T(1,128)} %bitcast.7), custom_call_target="tpu_custom_call" | custom-call | tf_op jit(solution)/shard_map/gcn_step/pallas_call | solution.py:469
  123.5 1.7 %gcn_finish.1 = (f32[1,1]{1,0:T(1,128)}, f32[128,256]{1,0:T(8,128)}, f32[40,256]{1,0:T(8,128)}) custom-call(f32[352,128]{1,0:T(8,128)} %gcn_step.1.sums), custom_call_target="tpu_custom_call" | custom-call | tf_op jit(solution)/shard_map/gcn_finish/pallas_call | solution.py:479

commit v4 on v3

--- a/solution.py
+++ b/solution.py
@@ -99,12 +99,8 @@
     ]
     for load in loads:
         load.start()
-    for n in range(4):
-        for e in range(2):
-            kept_copy(n, e).start()
-    for n in range(SLOTS):
-        for e in range(2):
-            slab_copy(n, e).start()
+    for e in range(2):
+        kept_copy(0, e).start()
 
     barrier = pltpu.get_barrier_semaphore()
     for dev in (pair, x_next, y_next):
@@ -154,6 +150,9 @@
 
     loads[0].wait()
     send_own(0, feats_all)
+    for e in range(2):
+        kept_copy(1, e).start()
+        kept_copy(2, e).start()
     for load in loads[1:]:
         load.wait()
     count[0] = jnp.full((8, 128), jnp.sum(mask_v[...].astype(F32)), F32)
@@ -183,6 +182,17 @@
             at = pl.ds(m, M_CHUNK)
             acc_one[at, :] += _dot(adj_buf[slot, at, :], right)
         fetch(s - 4 + SLOTS)
+
+        @pl.when(s == 0)
+        def _():
+            for e in range(2):
+                kept_copy(3, e).start()
+
+        @pl.when((s >= 1) & (s < 1 + SLOTS))
+        def _():
+            for e in range(2):
+                slab_copy(s - 1, e).start()
+
         return carry
 
     lax.fori_loop(0, 16, step_one, 0)
@@ -279,17 +289,16 @@
         stage[lax.rem(u, 4)] = _dot(back_t[...], adj_buf[slots[0], :, pl.ds(cols[0], quarter)])
         pair_move(u).start()
 
+        @pl.when(u >= 1)
+        def _():
+            finish(u - 1)
+
         @pl.when(u < 12)
         def _():
             part_copy(r, 1).wait()
 
         own_part[lax.rem(u, 2)] = _dot(back_t[...], adj_buf[slots[1], :, pl.ds(cols[1], quarter)])
         fetch(r + SLOTS)
-
-        @pl.when(u >= 1)
-        def _():
-            finish(u - 1)
-
         return carry
 
     lax.fori_loop(0, 16, step_three, 0)

time: 125 us -> 119 us (0.952)
  Pallas kernels: 125 us -> 118 us
    pallas_call x1, Pallas kernels: 123 us -> 116 us  [step(): pl.pallas_call(_kernel, out_shape=jax.ShapeDtypeStruct((352, 128), F32),...]
where the time goes in v4:
time: 119 us; the launch traced here: 118 us
  Pallas kernels  118 us (99%)
    pallas_call x1, Pallas kernels, step(): pl.pallas_call(_kernel, out_shape=jax.ShapeDtypeStruct((352, 128), F32),...  116 us

profile of v4, /device:TPU:0, one launch (start us, length us, event | category | flops | bytes accessed | tf_op | source)
XLA Modules:
  0.0 118.5 jit_solution(4326631577794694811)
XLA Ops:
  0.6 116.2 %gcn_step.1.sums = f32[352,128]{1,0:T(8,128)} custom-call(bf16[2048,16384]{1,0:T(8,128)(2,1)} %adj.1, bf16[2048,128]{1,0:T(8,128)(2,1)} %feat.1, f32[128,256]{1,0:T(8,128)} %w_one.1, f32[40,256]{1,0:T(8,128)} %bitcast.5, s32[1,2048]{1,0:T(1,128)} %bitcast.6, s32[1,2048]{1,0:T(1,128)} %bitcast.7), custom_call_target="tpu_custom_call" | custom-call | tf_op jit(solution)/shard_map/gcn_step/pallas_call | solution.py:478
  116.8 1.7 %gcn_finish.1 = (f32[1,1]{1,0:T(1,128)}, f32[128,256]{1,0:T(8,128)}, f32[40,256]{1,0:T(8,128)}) custom-call(f32[352,128]{1,0:T(8,128)} %gcn_step.1.sums), custom_call_target="tpu_custom_call" | custom-call | tf_op jit(solution)/shard_map/gcn_finish/pallas_call | solution.py:488

commit v5 on v4

--- a/solution.py
+++ b/solution.py
@@ -12,6 +12,7 @@
 
 SLOTS = 3
 M_CHUNK = 512
+M_TWO = 512
 
 
 def _dot(a, b):
@@ -25,7 +26,7 @@
 def _kernel(
     adj, feat, w_one, w_two, labels, mask,
     out,
-    feats_all, aggs_all, hid, acc_one, acc_two, agg_two, back_t, grad_t, pre_t,
+    feats_all, aggs_all, hid, hid_next, acc_one, acc_two, agg_two, back_t, grad_t, pre_t,
     own_part, own_sums, stage, from_pair, to_chip, from_chip, adj_buf,
     w_one_f, w_two_f, w_one_b, w_one_t, w_two_b, w_two_t, lab_v, mask_v, count, count_in,
     red, red_pair, red_link, red_next, red_last, red_out, small, small_in,
@@ -200,12 +201,12 @@
     aggs_all[me] = acc_one[...].astype(BF16)
     send_own(1, aggs_all)
 
-    def hidden_step(s):
+    def hidden_step(s, dst):
         for e in range(2):
             pre = _dot(piece(aggs_all, s, e)[...], w_one_b[...])
-            hid[lax.rem(s, 2), pl.ds(e * quarter, quarter), :] = jnp.maximum(pre, 0.0).astype(BF16)
-
-    def step_two(s, carry):
+            dst[pl.ds(e * quarter, quarter), :] = jnp.maximum(pre, 0.0).astype(BF16)
+
+    def step_two(s, now, then):
         @pl.when(s < 15)
         def _():
             gather_step(1, aggs_all, s + 1)
@@ -218,21 +219,24 @@
             for e in range(2):
                 adj_copy(gather_place(s, e), slot, e).wait()
 
-        hidden_step(jnp.minimum(s + 1, 15))
-        right = hid[lax.rem(s, 2)]
-        for m in range(0, rows, M_CHUNK):
-            at = pl.ds(m, M_CHUNK)
+        hidden_step(jnp.minimum(s + 1, 15), then)
+        right = now[...]
+        for m in range(0, rows, M_TWO):
+            at = pl.ds(m, M_TWO)
             acc_two[at, :] += _dot(adj_buf[slot, at, :], right)
 
         @pl.when(s >= 4)
         def _():
             fetch(s + 8 + SLOTS)
 
+    def two_steps(i, carry):
+        step_two(2 * i, hid, hid_next)
+        step_two(2 * i + 1, hid_next, hid)
         return carry
 
     gather_step(1, aggs_all, jnp.int32(0))
-    hidden_step(jnp.int32(0))
-    lax.fori_loop(0, 16, step_two, 0)
+    hidden_step(jnp.int32(0), hid)
+    lax.fori_loop(0, 8, two_steps, 0)
 
     count_move(2).wait_recv()
     total = (count[2] + count_in[2])[0:1, 0:1]
@@ -426,7 +430,8 @@
         scratch = [
             pltpu.VMEM((parts, rows, feat_dim), BF16),
             pltpu.VMEM((parts, rows, feat_dim), BF16),
-            pltpu.VMEM((2, rows // 2, hidden), BF16),
+            pltpu.VMEM((rows // 2, hidden), BF16),
+            pltpu.VMEM((rows // 2, hidden), BF16),
             pltpu.VMEM((rows, feat_dim), F32),
             pltpu.VMEM((rows, hidden), F32),
             pltpu.VMEM((rows, hidden), BF16),

time: 119 us -> 117 us (0.983)
  no operation moved by 1% of the time
where the time goes in v5:
time: 117 us
  Pallas kernels  117 us (100%)
    pallas_call x1, Pallas kernels, step(): pl.pallas_call(_kernel, out_shape=jax.ShapeDtypeStruct((352, 128), F32),...  115 us

profile of v5, /device:TPU:0, one launch (start us, length us, event | category | flops | bytes accessed | tf_op | source)
XLA Modules:
  0.0 117.3 jit_solution(7569093290465601175)
XLA Ops:
  0.6 115.0 %gcn_step.1.sums = f32[352,128]{1,0:T(8,128)} custom-call(bf16[2048,16384]{1,0:T(8,128)(2,1)} %adj.1, bf16[2048,128]{1,0:T(8,128)(2,1)} %feat.1, f32[128,256]{1,0:T(8,128)} %w_one.1, f32[40,256]{1,0:T(8,128)} %bitcast.5, s32[1,2048]{1,0:T(1,128)} %bitcast.6, s32[1,2048]{1,0:T(1,128)} %bitcast.7), custom_call_target="tpu_custom_call" | custom-call | tf_op jit(solution)/shard_map/gcn_step/pallas_call | solution.py:483
  115.6 1.7 %gcn_finish.1 = (f32[1,1]{1,0:T(1,128)}, f32[128,256]{1,0:T(8,128)}, f32[40,256]{1,0:T(8,128)}) custom-call(f32[352,128]{1,0:T(8,128)} %gcn_step.1.sums), custom_call_target="tpu_custom_call" | custom-call | tf_op jit(solution)/shard_map/gcn_finish/pallas_call | solution.py:493

commit v6 on v5

--- a/solution.py
+++ b/solution.py
@@ -274,38 +274,48 @@
         def _():
             own_sums[u - 12] = both
 
-    def step_three(u, carry):
+    def make_part(u, which):
         r = u + 24
         ring = 1 - u // 12
         kept = (1 - ring) * (u - 12)
-        slots = [ring * lax.rem(r, SLOTS) + (1 - ring) * (SLOTS + 2 * (1 - e) + kept // 2) for e in range(2)]
-        cols = [pl.multiple_of((ring * e + lax.rem(kept, 2)) * quarter, quarter) for e in range(2)]
-
+        slot = ring * lax.rem(r, SLOTS) + (1 - ring) * (SLOTS + 2 * (1 - which) + kept // 2)
+        col = pl.multiple_of((ring * which + lax.rem(kept, 2)) * quarter, quarter)
+
+        @pl.when(u < 12)
+        def _():
+            part_copy(r, which).wait()
+
+        part = _dot(back_t[...], adj_buf[slot, :, pl.ds(col, quarter)])
+        if which == 0:
+            stage[lax.rem(u, 4)] = part
+            pair_move(u).start()
+        else:
+            own_part[lax.rem(u, 2)] = part
+            fetch(r + SLOTS)
+
+    def step_three(u, carry):
         @pl.when(u >= 4)
         def _():
             pair_move(u).wait_send()
             pl.semaphore_wait(pair_free, 1)
 
-        @pl.when(u < 12)
-        def _():
-            part_copy(r, 0).wait()
-
-        stage[lax.rem(u, 4)] = _dot(back_t[...], adj_buf[slots[0], :, pl.ds(cols[0], quarter)])
-        pair_move(u).start()
-
-        @pl.when(u >= 1)
+        make_part(u, 0)
+
+        @pl.when(u >= 3)
         def _():
             finish(u - 1)
 
-        @pl.when(u < 12)
-        def _():
-            part_copy(r, 1).wait()
-
-        own_part[lax.rem(u, 2)] = _dot(back_t[...], adj_buf[slots[1], :, pl.ds(cols[1], quarter)])
-        fetch(r + SLOTS)
+        make_part(u, 1)
         return carry
 
-    lax.fori_loop(0, 16, step_three, 0)
+    first, second = jnp.int32(0), jnp.int32(1)
+    make_part(first, 0)
+    make_part(second, 0)
+    make_part(first, 1)
+    finish(first)
+    make_part(second, 1)
+    finish(second)
+    lax.fori_loop(2, 16, step_three, 0)
     finish(jnp.int32(15))
     for u in range(12, 16):
         pair_move(u).wait_send()

time: 117 us -> 117 us (level)
  no operation moved by 1% of the time
where the time goes in v6:
time: 117 us
  Pallas kernels  116 us (99%)
    pallas_call x1, Pallas kernels, step(): pl.pallas_call(_kernel, out_shape=jax.ShapeDtypeStruct((352, 128), F32),...  115 us

profile of v6, /device:TPU:0, one launch (start us, length us, event | category | flops | bytes accessed | tf_op | source)
XLA Modules:
  0.0 117.1 jit_solution(9687269127831162962)
XLA Ops:
  0.6 114.8 %gcn_step.1.sums = f32[352,128]{1,0:T(8,128)} custom-call(bf16[2048,16384]{1,0:T(8,128)(2,1)} %adj.1, bf16[2048,128]{1,0:T(8,128)(2,1)} %feat.1, f32[128,256]{1,0:T(8,128)} %w_one.1, f32[40,256]{1,0:T(8,128)} %bitcast.5, s32[1,2048]{1,0:T(1,128)} %bitcast.6, s32[1,2048]{1,0:T(1,128)} %bitcast.7), custom_call_target="tpu_custom_call" | custom-call | tf_op jit(solution)/shard_map/gcn_step/pallas_call | solution.py:493
  115.5 1.7 %gcn_finish.1 = (f32[1,1]{1,0:T(1,128)}, f32[128,256]{1,0:T(8,128)}, f32[40,256]{1,0:T(8,128)}) custom-call(f32[352,128]{1,0:T(8,128)} %gcn_step.1.sums), custom_call_target="tpu_custom_call" | custom-call | tf_op jit(solution)/shard_map/gcn_finish/pallas_call | solution.py:503

commit v7 on v6

--- a/solution.py
+++ b/solution.py
@@ -207,8 +207,7 @@
             dst[pl.ds(e * quarter, quarter), :] = jnp.maximum(pre, 0.0).astype(BF16)
 
     def step_two(s, now, then):
-        @pl.when(s < 15)
-        def _():
+        if then is not None:
             gather_step(1, aggs_all, s + 1)
 
         kept = 1 - (s + 12) // 16
@@ -219,7 +218,8 @@
             for e in range(2):
                 adj_copy(gather_place(s, e), slot, e).wait()
 
-        hidden_step(jnp.minimum(s + 1, 15), then)
+        if then is not None:
+            hidden_step(s + 1, then)
         right = now[...]
         for m in range(0, rows, M_TWO):
             at = pl.ds(m, M_TWO)
@@ -236,7 +236,9 @@
 
     gather_step(1, aggs_all, jnp.int32(0))
     hidden_step(jnp.int32(0), hid)
-    lax.fori_loop(0, 8, two_steps, 0)
+    lax.fori_loop(0, 7, two_steps, 0)
+    step_two(jnp.int32(14), hid, hid_next)
+    step_two(jnp.int32(15), hid_next, None)
 
     count_move(2).wait_recv()
     total = (count[2] + count_in[2])[0:1, 0:1]
@@ -325,8 +327,13 @@
     small[0, 40:80, :] = part_two[0:classes, 128:256]
     small[0, 80:96, :] = jnp.full((16, 128), loss_sum, F32)
 
+    share = pl.ds(pl.multiple_of(core * 48, 8), 48)
+    others = pl.ds(pl.multiple_of((1 - core) * 48, 8), 48)
+
     def small_move(i):
-        return remote(small.at[i], small_in.at[i], small_send.at[i], small_recv.at[i], (pair, x_next, y_next)[i])
+        at = pl.ds(0, 96) if i == 0 else share
+        return remote(small.at[i, at], small_in.at[i, at], small_send.at[i], small_recv.at[i],
+                      (pair, x_next, y_next)[i])
 
     small_move(0).start()
     pre_t[...] = _dot_nt(w_one_t[...], aggs_all[me])
@@ -349,7 +356,7 @@
             chip_move(4 + 2 * j + link).wait_recv()
             own_sums[j] += from_chip[link, 2 + j].astype(F32)
     small_move(1).wait_recv()
-    small[2] = small[1] + small_in[1]
+    small[2, share, :] = small[1, share, :] + small_in[1, share, :]
     small_move(2).start()
     red_one = jnp.zeros((256, 128), F32)
     for k in range(2):
@@ -395,17 +402,20 @@
     ref = red_out.at[pl.ds(mine, n_half)]
     back = remote(ref, ref, red_send.at[5], red_recv.at[5], pair)
     back.start()
+    small_move(2).wait_recv()
+    small[3, share, :] = small[2, share, :] + small_in[2, share, :]
+    small_back = remote(small.at[3, share], small.at[3, share], small_send.at[3], small_recv.at[3], pair)
+    small_back.start()
+    remote(small.at[3, others], small.at[3, others], small_send.at[3], small_recv.at[3], pair).wait_recv()
     ref_in = red_out.at[pl.ds(other, n_half)]
     remote(ref_in, ref_in, red_send.at[5], red_recv.at[5], pair).wait_recv()
 
-    small_move(2).wait_recv()
-    summed = small[2] + small_in[2]
     out[0:256, :] = red_out[...]
-    out[256:336, :] = summed[0:80, :]
-    out[336:352, :] = summed[80:96, :] / total
+    out[256:336, :] = small[3, 0:80, :]
+    out[336:352, :] = small[3, 80:96, :] / total
 
     move.wait_send()
-    for m in moves + lasts + [back]:
+    for m in moves + lasts + [back, small_back]:
         m.wait_send()
     for i in range(3):
         count_move(i).wait_send()
@@ -471,7 +481,7 @@
             pltpu.VMEM((128, 128), F32),
             pltpu.VMEM((2, 128, 128), F32),
             pltpu.VMEM((256, 128), F32),
-            pltpu.VMEM((3, 96, 128), F32),
+            pltpu.VMEM((4, 96, 128), F32),
             pltpu.VMEM((3, 96, 128), F32),
             pltpu.SemaphoreType.DMA((SLOTS + 4, 2)),
             pltpu.SemaphoreType.DMA((5,)),
@@ -486,8 +496,8 @@
             pltpu.SemaphoreType.DMA((2, 8)),
             pltpu.SemaphoreType.DMA((6,)),
             pltpu.SemaphoreType.DMA((6,)),
-            pltpu.SemaphoreType.DMA((3,)),
-            pltpu.SemaphoreType.DMA((3,)),
+            pltpu.SemaphoreType.DMA((4,)),
+            pltpu.SemaphoreType.DMA((4,)),
             pltpu.SemaphoreType.DMA((2, 2)),
         ]
         sums = pl.pallas_call(

time: 117 us -> 116 us (level)
    pallas_call x1, Pallas kernels: 115 us -> 113 us  [step(): pl.pallas_call(_kernel, out_shape=jax.ShapeDtypeStruct((352, 128), F32),...]
where the time goes in v7:
time: 116 us
  Pallas kernels  115 us (99%)
    pallas_call x1, Pallas kernels, step(): pl.pallas_call(_kernel, out_shape=jax.ShapeDtypeStruct((352, 128), F32),...  113 us

profile of v7, /device:TPU:0, one launch (start us, length us, event | category | flops | bytes accessed | tf_op | source)
XLA Modules:
  0.0 115.8 jit_solution(5796325840310803725)
XLA Ops:
  0.6 113.5 %gcn_step.1.sums = f32[352,128]{1,0:T(8,128)} custom-call(bf16[2048,16384]{1,0:T(8,128)(2,1)} %adj.1, bf16[2048,128]{1,0:T(8,128)(2,1)} %feat.1, f32[128,256]{1,0:T(8,128)} %w_one.1, f32[40,256]{1,0:T(8,128)} %bitcast.5, s32[1,2048]{1,0:T(1,128)} %bitcast.6, s32[1,2048]{1,0:T(1,128)} %bitcast.7), custom_call_target="tpu_custom_call" | custom-call | tf_op jit(solution)/shard_map/gcn_step/pallas_call | solution.py:503
  114.1 1.7 %gcn_finish.1 = (f32[1,1]{1,0:T(1,128)}, f32[128,256]{1,0:T(8,128)}, f32[40,256]{1,0:T(8,128)}) custom-call(f32[352,128]{1,0:T(8,128)} %gcn_step.1.sums), custom_call_target="tpu_custom_call" | custom-call | tf_op jit(solution)/shard_map/gcn_finish/pallas_call | solution.py:513

commit v8 on v7

--- a/solution.py
+++ b/solution.py
@@ -11,7 +11,7 @@
 BF16 = jnp.bfloat16
 
 SLOTS = 3
-M_CHUNK = 512
+M_CHUNK = 256
 M_TWO = 512
 
 
@@ -340,7 +340,6 @@
 
     small_move(0).wait_recv()
     small[1] = small[0] + small_in[0]
-    small_move(1).start()
 
     relays = []
     for k in range(2):
@@ -350,14 +349,12 @@
                           chip_recv.at[1 - link, 6 + k], (y_next, x_next)[link])
             move.start()
             relays.append(move)
+    small_move(1).start()
 
     for j in range(4):
         for link in range(2):
             chip_move(4 + 2 * j + link).wait_recv()
             own_sums[j] += from_chip[link, 2 + j].astype(F32)
-    small_move(1).wait_recv()
-    small[2, share, :] = small[1, share, :] + small_in[1, share, :]
-    small_move(2).start()
     red_one = jnp.zeros((256, 128), F32)
     for k in range(2):
         for link in range(2):
@@ -376,6 +373,9 @@
 
     move = remote(red.at[pl.ds(other, n_half)], red_pair, red_send.at[0], red_recv.at[0], pair)
     move.start()
+    small_move(1).wait_recv()
+    small[2, share, :] = small[1, share, :] + small_in[1, share, :]
+    small_move(2).start()
     move.wait_recv()
     red_link[...] = red[pl.ds(mine, n_half), :] + red_pair[...]
     moves = [

time: 116 us -> 116 us (level)
  no operation moved by 1% of the time
where the time goes in v8:
time: 116 us
  Pallas kernels  115 us (99%)
    pallas_call x1, Pallas kernels, step(): pl.pallas_call(_kernel, out_shape=jax.ShapeDtypeStruct((352, 128), F32),...  113 us

profile of v8, /device:TPU:0, one launch (start us, length us, event | category | flops | bytes accessed | tf_op | source)
XLA Modules:
  0.0 115.6 jit_solution(3256834176079622246)
XLA Ops:
  0.6 113.3 %gcn_step.1.sums = f32[352,128]{1,0:T(8,128)} custom-call(bf16[2048,16384]{1,0:T(8,128)(2,1)} %adj.1, bf16[2048,128]{1,0:T(8,128)(2,1)} %feat.1, f32[128,256]{1,0:T(8,128)} %w_one.1, f32[40,256]{1,0:T(8,128)} %bitcast.5, s32[1,2048]{1,0:T(1,128)} %bitcast.6, s32[1,2048]{1,0:T(1,128)} %bitcast.7), custom_call_target="tpu_custom_call" | custom-call | tf_op jit(solution)/shard_map/gcn_step/pallas_call | solution.py:503
  114.0 1.7 %gcn_finish.1 = (f32[1,1]{1,0:T(1,128)}, f32[128,256]{1,0:T(8,128)}, f32[40,256]{1,0:T(8,128)}) custom-call(f32[352,128]{1,0:T(8,128)} %gcn_step.1.sums), custom_call_target="tpu_custom_call" | custom-call | tf_op jit(solution)/shard_map/gcn_finish/pallas_call | solution.py:513

commit v9 on v8

--- a/solution.py
+++ b/solution.py
@@ -107,8 +107,6 @@
     for dev in (pair, x_next, y_next):
         pl.semaphore_signal(barrier, inc=1, device_id=(dev,), device_id_type=MESH)
     acc_one[...] = jnp.zeros_like(acc_one)
-    acc_two[...] = jnp.zeros_like(acc_two)
-    grad_t[...] = jnp.zeros_like(grad_t)
     pl.semaphore_wait(barrier, 3)
 
     def piece(buf, s, e):
@@ -154,6 +152,8 @@
     for e in range(2):
         kept_copy(1, e).start()
         kept_copy(2, e).start()
+    acc_two[...] = jnp.zeros_like(acc_two)
+    grad_t[...] = jnp.zeros_like(grad_t)
     for load in loads[1:]:
         load.wait()
     count[0] = jnp.full((8, 128), jnp.sum(mask_v[...].astype(F32)), F32)

time: 116 us -> 116 us (level)
  no operation moved by 1% of the time
where the time goes in v9:
time: 116 us
  Pallas kernels  115 us (99%)
    pallas_call x1, Pallas kernels, step(): pl.pallas_call(_kernel, out_shape=jax.ShapeDtypeStruct((352, 128), F32),...  113 us

profile of v9, /device:TPU:0, one launch (start us, length us, event | category | flops | bytes accessed | tf_op | source)
XLA Modules:
  0.0 115.6 jit_solution(9597125101359102264)
XLA Ops:
  0.6 113.3 %gcn_step.1.sums = f32[352,128]{1,0:T(8,128)} custom-call(bf16[2048,16384]{1,0:T(8,128)(2,1)} %adj.1, bf16[2048,128]{1,0:T(8,128)(2,1)} %feat.1, f32[128,256]{1,0:T(8,128)} %w_one.1, f32[40,256]{1,0:T(8,128)} %bitcast.5, s32[1,2048]{1,0:T(1,128)} %bitcast.6, s32[1,2048]{1,0:T(1,128)} %bitcast.7), custom_call_target="tpu_custom_call" | custom-call | tf_op jit(solution)/shard_map/gcn_step/pallas_call | solution.py:503
  114.0 1.7 %gcn_finish.1 = (f32[1,1]{1,0:T(1,128)}, f32[128,256]{1,0:T(8,128)}, f32[40,256]{1,0:T(8,128)}) custom-call(f32[352,128]{1,0:T(8,128)} %gcn_step.1.sums), custom_call_target="tpu_custom_call" | custom-call | tf_op jit(solution)/shard_map/gcn_finish/pallas_call | solution.py:513
